TPU v7x, 8 devices: a whole 2x2x1 slice. The times are simulated.
8 devices in a mesh: tp: 4 (over z, y, x), ep: 2 (over core).
Axes of the slice: x: 2, y: 2, z: 1, core: 2. Of those that a mesh axis runs over, the one named last changes fastest.
Arguments:
- x: bfloat16 [8192, 2048], P(('ep', 'tp'))
- y_grad: bfloat16 [8192, 2048], P(('ep', 'tp'))
- expert_ids: int32 [8192, 2], P(('ep', 'tp'))
- norm_gain: bfloat16 [2048], replicated
- w_router: bfloat16 [2048, 8], replicated
- w_gate: bfloat16 [8, 2048, 5632], P('ep', None, 'tp')
- w_up: bfloat16 [8, 2048, 5632], P('ep', None, 'tp')
- w_down: bfloat16 [8, 5632, 2048], P('ep', 'tp')
Outputs:
- output 1: bfloat16 [8192, 2048], P(('ep', 'tp'))
- output 2: bfloat16 [8192, 2048], P(('ep', 'tp'))
- output 3: bfloat16 [2048], replicated
- output 4: bfloat16 [2048, 8], replicated
- output 5: bfloat16 [8, 2048, 5632], P('ep', None, 'tp')
- output 6: bfloat16 [8, 2048, 5632], P('ep', None, 'tp')
- output 7: bfloat16 [8, 5632, 2048], P('ep', 'tp')
- output 8: float32 [], replicated
- output 9: float32 [], replicated
All inputs are finite; a program needn't handle non-finite values.
Results may differ from a plain program's by a relative error of at most 0.0154491.
Values are sent between devices in bfloat16 or wider.
A program may use at most 1 GiB of HBM per device.

v0:
```python
import jax
import jax.numpy as jnp
from jax import lax
from jax.sharding import PartitionSpec as P

NORM_EPS = 1e-6
ACT_COEF = 1e-5
BALANCE_COEF = 1e-3


def solution(mesh):
    tp_size = mesh.shape["tp"]
    ep_size = mesh.shape["ep"]
    dev_count = tp_size * ep_size
    all_axes = ("tp", "ep")
    row_spec = P(("ep", "tp"), None)
    wide_spec = P("ep", None, "tp")
    down_spec = P("ep", "tp", None)

    def body(x, y_grad, expert_ids, norm_gain, w_router, w_gate, w_up, w_down):
        tokens, model_dim = x.shape
        top_k = expert_ids.shape[1]
        num_experts = w_router.shape[1]
        local_experts = w_gate.shape[0]
        capacity = 2 * top_k * tokens // num_experts
        total_tokens = tokens * dev_count
        assign_count = tokens * top_k

        flat_ids = expert_ids.reshape(-1)
        expert_range = jnp.arange(num_experts, dtype=jnp.int32)
        id_hot = (flat_ids[:, None] == expert_range[None, :]).astype(jnp.int32)
        position = jnp.sum((jnp.cumsum(id_hot, axis=0) - 1) * id_hot, axis=1)
        slot = flat_ids * capacity + position
        assign_of_slot = jax.ops.segment_sum(jnp.arange(assign_count, dtype=jnp.int32) - assign_count, slot, num_segments=num_experts * capacity) + assign_count
        token_of_slot = assign_of_slot // top_k
        choice = (expert_ids[:, :, None] == expert_range[None, None, :]).astype(jnp.float32)

        def to_experts(rows):
            sent = lax.all_to_all(rows.reshape(ep_size, local_experts, capacity, model_dim), "ep", 0, 2, tiled=True)
            return lax.all_gather(sent.reshape(local_experts, ep_size * capacity, model_dim), "tp", axis=1, tiled=True)

        def from_experts(part_rows):
            summed = lax.psum_scatter(part_rows, "tp", scatter_dimension=1, tiled=True)
            returned = lax.all_to_all(summed.reshape(1, local_experts, ep_size * capacity, model_dim), "ep", 2, 0, tiled=True)
            return returned.reshape(num_experts * capacity, model_dim)

        x_float = x.astype(jnp.float32)
        inv_rms = lax.rsqrt(jnp.mean(x_float * x_float, axis=-1, keepdims=True) + NORM_EPS)
        unit = x_float * inv_rms
        gain = norm_gain.astype(jnp.float32)
        x_norm = (unit * gain).astype(jnp.bfloat16)
        route_prob = jax.nn.softmax(jnp.dot(x_norm, w_router, preferred_element_type=jnp.float32), axis=-1)
        gates = jnp.sum(choice * route_prob[:, None, :], axis=-1)
        route_stats = lax.psum(jnp.stack([jnp.sum(choice, axis=(0, 1)), jnp.sum(route_prob, axis=0)]), all_axes)
        counts = route_stats[0]
        balance_scale = BALANCE_COEF * num_experts / (total_tokens * total_tokens * top_k)
        balance_loss = balance_scale * jnp.sum(counts * route_stats[1])

        rows_in = to_experts(jnp.take(x_norm, token_of_slot, axis=0, mode="fill", fill_value=0))
        pre_gate = jnp.einsum("ecd,edf->ecf", rows_in, w_gate, preferred_element_type=jnp.float32)
        pre_up = jnp.einsum("ecd,edf->ecf", rows_in, w_up, preferred_element_type=jnp.float32)
        gate_sig = jax.nn.sigmoid(pre_gate)
        silu_gate = pre_gate * gate_sig
        hidden = (silu_gate * pre_up).astype(jnp.bfloat16)
        out_part = jnp.einsum("ecf,efd->ecd", hidden, w_down, preferred_element_type=jnp.float32).astype(jnp.bfloat16)
        picked = jnp.take(from_experts(out_part), slot, axis=0).reshape(tokens, top_k, model_dim)
        moe_out = jnp.sum(gates[:, :, None] * picked.astype(jnp.float32), axis=1)
        y = (x_float + moe_out).astype(jnp.bfloat16)
        act_loss = ACT_COEF * lax.psum(jnp.sum(moe_out * moe_out), all_axes) / (total_tokens * model_dim)

        moe_grad = y_grad.astype(jnp.float32) + (2.0 * ACT_COEF / (total_tokens * model_dim)) * moe_out
        gate_weight_grad = jnp.sum(moe_grad[:, None, :] * picked.astype(jnp.float32), axis=-1)
        picked_grad = (gates[:, :, None] * moe_grad[:, None, :]).astype(jnp.bfloat16).reshape(assign_count, model_dim)
        rows_grad = to_experts(jnp.take(picked_grad, assign_of_slot, axis=0, mode="fill", fill_value=0))
        hidden_grad = jnp.einsum("ecd,efd->ecf", rows_grad, w_down, preferred_element_type=jnp.float32)
        down_grad = jnp.einsum("ecf,ecd->efd", hidden, rows_grad, preferred_element_type=jnp.float32).astype(jnp.bfloat16)
        pre_up_grad = (hidden_grad * silu_gate).astype(jnp.bfloat16)
        pre_gate_grad = (hidden_grad * pre_up * gate_sig * (1.0 + pre_gate * (1.0 - gate_sig))).astype(jnp.bfloat16)
        gate_grad = jnp.einsum("ecd,ecf->edf", rows_in, pre_gate_grad, preferred_element_type=jnp.float32).astype(jnp.bfloat16)
        up_grad = jnp.einsum("ecd,ecf->edf", rows_in, pre_up_grad, preferred_element_type=jnp.float32).astype(jnp.bfloat16)
        in_part_grad = (jnp.einsum("ecf,edf->ecd", pre_gate_grad, w_gate, preferred_element_type=jnp.float32) + jnp.einsum("ecf,edf->ecd", pre_up_grad, w_up, preferred_element_type=jnp.float32)).astype(jnp.bfloat16)
        returned_grad = jnp.take(from_experts(in_part_grad), slot, axis=0).reshape(tokens, top_k, model_dim)
        x_norm_grad = jnp.sum(returned_grad.astype(jnp.float32), axis=1)
        prob_grad = jnp.sum(gate_weight_grad[:, :, None] * choice, axis=1) + balance_scale * counts[None, :]
        logit_grad = (route_prob * (prob_grad - jnp.sum(route_prob * prob_grad, axis=-1, keepdims=True))).astype(jnp.bfloat16)
        x_norm_grad = x_norm_grad + jnp.einsum("se,de->sd", logit_grad, w_router, preferred_element_type=jnp.float32)
        unit_grad = x_norm_grad * gain
        x_grad = y_grad.astype(jnp.float32) + inv_rms * (unit_grad - unit * jnp.mean(unit_grad * unit, axis=-1, keepdims=True))
        gain_sum, router_sum = lax.psum((jnp.sum(x_norm_grad * unit, axis=0), jnp.einsum("sd,se->de", x_norm, logit_grad, preferred_element_type=jnp.float32)), all_axes)
        return (y, x_grad.astype(jnp.bfloat16), gain_sum.astype(jnp.bfloat16), router_sum.astype(jnp.bfloat16), gate_grad, up_grad, down_grad, balance_loss, act_loss)

    return jax.shard_map(body, mesh=mesh, in_specs=(row_spec, row_spec, row_spec, P(), P(), wide_spec, wide_spec, down_spec), out_specs=(row_spec, row_spec, P(), P(), wide_spec, wide_spec, down_spec, P(), P()), check_vma=False)
```

profile of v0, /device:TPU:0, one launch (start us, length us, event | category | flops | bytes accessed | tf_op | source)
XLA Modules:
  0.0 3548.8 jit_solution(16444604217680065741)
XLA Ops:
  35.0 34.0 gather_fusion
  77.4 17.7 all_to_all.60
  102.2 573.2 %all-gather.3.cloned.1.call-done = bf16[4,4096,2048]{2,1,0:T(8,128)(2,1)} async-done(((bf16[4,1024,2048]{2,1,0:T(8,128)(2,1)}), bf16[4,4096,2048]{2,1,0:T(8,128)(2,1)}) %all-gather.3.cloned.1.call-update) | async-done | bytes 67108880 | tf_op jit(solution)/shard_map/all_gather | solution.py:40
  675.4 115.3 %fusion.26 = f32[4,4096,1408]{2,1,0:T(8,128)} fusion(bf16[4,4096,2048]{2,1,0:T(8,128)(2,1)} %all-gather.3.cloned.1.call-done, bf16[4,2048,1408]{2,1,0:T(8,128)(2,1)} %param.15), kind=kOutput, calls=%fused_computation.85 | convolution fusion | flops 94489280512 | bytes 182452224 | tf_op jit(solution)/shard_map/ecd,edf->ecf/dot_general | solution.py:60
  790.7 128.7 %multiply_convert_fusion.2 = (bf16[4,4096,1408]{2,1,0:T(8,128)(2,1)}, f32[4,4096,1408]{2,1,0:T(8,128)}) fusion(f32[4,4096,1408]{2,1,0:T(8,128)} %fusion.26, bf16[4,4096,2048]{2,1,0:T(8,128)(2,1)} %all-gather.3.cloned.1.call-done, bf16[4,2048,1408]{2,1,0:T(8,128)(2,1)} %param.16), kind=kOutput, calls=%fused_computation.8 | convolution fusion | flops 94627692544 | bytes 320864256 | tf_op jit(solution)/shard_map/ecd,edf->ecf/dot_general | solution.py:61
  919.4 113.8 %convolution_convert_fusion = bf16[4,4096,2048]{2,1,0:T(8,128)(2,1)} fusion(bf16[4,4096,1408]{2,1,0:T(8,128)(2,1)} %get-tuple-element.32, bf16[4,1408,2048]{2,1,0:T(8,128)(2,1)} %param.17), kind=kOutput, calls=%fused_computation.11 | convolution fusion | flops 94522834944 | bytes 136314880 | tf_op jit(solution)/shard_map/ecf,efd->ecd/dot_general | solution.py:65
  1039.8 546.0 %reduce-scatter.3.cloned.1.call-done = bf16[4,1024,2048]{2,1,0:T(8,128)(2,1)} async-done(((bf16[4,4096,2048]{2,1,0:T(8,128)(2,1)}), bf16[4,1024,2048]{2,1,0:T(8,128)(2,1)}) %reduce-scatter.3.cloned.1.call-update) | async-done | bytes 16777232 | tf_op jit(solution)/shard_map/reduce_scatter | solution.py:43
  1585.8 19.1 copy.59
  1604.9 17.7 all_to_all.61
  1622.6 21.1 copy.60
  1643.7 24.2 gather_fusion.2
  1678.6 20.0 reshape.149
  1698.6 29.3 multiply_reduce_fusion.1
  1750.3 20.7 mul.187
  1784.0 35.8 %gather_fusion.1 = bf16[4096,2048]{1,0:T(8,128)(2,1)} fusion(bf16[2048,2048]{1,0:T(8,128)(2,1)} %get-tuple-element.22, s32[4096]{0:T(1024)S(1)} %copy-done.18), kind=kCustom, calls=%fused_computation.3 | custom fusion | bytes 33570816 | tf_op jit(solution)/shard_map/jit(_take)/gather | solution.py:74
  1828.2 17.3 all_to_all.62
  1852.1 571.2 %all-gather.5.cloned.1.call-done = bf16[4,4096,2048]{2,1,0:T(8,128)(2,1)} async-done(((bf16[4,1024,2048]{2,1,0:T(8,128)(2,1)}), bf16[4,4096,2048]{2,1,0:T(8,128)(2,1)}) %all-gather.5.cloned.1.call-update) | async-done | bytes 67108880 | tf_op jit(solution)/shard_map/all_gather | solution.py:40
  2423.3 149.5 %multiply_convert_fusion = (bf16[4,4096,1408]{2,1,0:T(8,128)(2,1)}, bf16[4,4096,1408]{2,1,0:T(8,128)(2,1)}) fusion(f32[4,4096,1408]{2,1,0:T(8,128)} %fusion.26, f32[4,4096,1408]{2,1,0:T(8,128)} %get-tuple-element.33, bf16[4,4096,2048]{2,1,0:T(8,128)(2,1)} %all-gather.5.cloned.1.call-done, bf16[4,1408,2048]{2,1,0:T(8,128)(2,1)} %param.17), kind=kOutput, calls=%fused_computation.6 | convolution fusion | flops 94789173248 | bytes 367001600 | tf_op jit(solution)/shard_map/ecd,efd->ecf/dot_general | solution.py:75
  2572.7 115.5 %fusion.27 = f32[4,4096,2048]{2,1,0:T(8,128)} fusion(bf16[4,4096,1408]{2,1,0:T(8,128)(2,1)} %get-tuple-element.20, bf16[4,2048,1408]{2,1,0:T(8,128)(2,1)} %param.15), kind=kOutput, calls=%fused_computation.86 | convolution fusion | flops 94489280512 | bytes 203423744 | tf_op jit(solution)/shard_map/ecf,edf->ecd/dot_general | solution.py:81
  2688.2 119.6 %add_convert_fusion = bf16[4,4096,2048]{2,1,0:T(8,128)(2,1)} fusion(f32[4,4096,2048]{2,1,0:T(8,128)} %fusion.27, bf16[4,4096,1408]{2,1,0:T(8,128)(2,1)} %get-tuple-element.19, bf16[4,2048,1408]{2,1,0:T(8,128)(2,1)} %param.16), kind=kOutput, calls=%fused_computation.5 | convolution fusion | flops 94556389376 | bytes 270532608 | tf_op jit(solution)/shard_map/ecf,edf->ecd/dot_general | solution.py:81
  2809.4 22.9 psum.28
  2837.2 105.7 %convolution_convert_fusion.1 = bf16[4,1408,2048]{2,1,0:T(8,128)(2,1)} fusion(bf16[4,4096,1408]{2,1,0:T(8,128)(2,1)} %get-tuple-element.32, bf16[4,4096,2048]{2,1,0:T(8,128)(2,1)} %all-gather.5.cloned.1.call-done), kind=kOutput, calls=%fused_computation.12 | convolution fusion | flops 94500814848 | bytes 136314880 | tf_op jit(solution)/shard_map/ecf,ecd->efd/dot_general | solution.py:76
  2942.9 114.9 %convolution_convert_fusion.2 = bf16[4,2048,1408]{2,1,0:T(8,128)(2,1)} fusion(bf16[4,4096,2048]{2,1,0:T(8,128)(2,1)} %all-gather.3.cloned.1.call-done, bf16[4,4096,1408]{2,1,0:T(8,128)(2,1)} %get-tuple-element.19), kind=kOutput, calls=%fused_computation.13 | convolution fusion | flops 94500814848 | bytes 136314880 | tf_op jit(solution)/shard_map/ecd,ecf->edf/dot_general | solution.py:80
  3057.8 114.7 %convolution_convert_fusion.3 = bf16[4,2048,1408]{2,1,0:T(8,128)(2,1)} fusion(bf16[4,4096,2048]{2,1,0:T(8,128)(2,1)} %all-gather.3.cloned.1.call-done, bf16[4,4096,1408]{2,1,0:T(8,128)(2,1)} %get-tuple-element.20), kind=kOutput, calls=%fused_computation.14 | convolution fusion | flops 94500814848 | bytes 136314880 | tf_op jit(solution)/shard_map/ecd,ecf->edf/dot_general | solution.py:79
  3172.5 189.2 %reduce-scatter.5.cloned.1.call-done = bf16[4,1024,2048]{2,1,0:T(8,128)(2,1)} async-done(((bf16[4,4096,2048]{2,1,0:T(8,128)(2,1)}), bf16[4,1024,2048]{2,1,0:T(8,128)(2,1)}) %reduce-scatter.5.cloned.1.call-update) | async-done | bytes 16777232 | tf_op jit(solution)/shard_map/reduce_scatter | solution.py:43
  3361.7 19.1 copy.63
  3380.8 17.5 all_to_all.63
  3398.3 21.1 copy.64
  3419.4 24.3 gather_fusion.3
  3453.9 20.0 reshape.150
  3473.9 24.7 reduce_sum.143
  3506.7 23.7 all-reduce
  (109 shorter events, 143.4 us)
Async XLA Ops:
  7.2 1027.3 %copy-start = (bf16[2048,8]{0,1:T(8,128)(2,1)S(1)}, bf16[2048,8]{0,1:T(8,128)(2,1)}, u32[]{:S(2)}) copy-start(bf16[2048,8]{0,1:T(8,128)(2,1)} %param.14) | copy-start | bytes 98308
  7.2 668.2 %all-gather.3.cloned.1.call-start = ((), (), s32[]{:S(2)}) async-start(), calls=%async_computation.6 | async-start | bytes 83886080 | tf_op jit(solution)/shard_map/all_gather | solution.py:40
  9.1 59.9 %copy-start.8 = (s32[2048]{0:T(1024)}, s32[2048]{0:T(1024)S(1)}, u32[]{:S(2)}) copy-start(s32[2048]{0:T(1024)S(1)} %eq.41) | copy-start | bytes 24580
  12.9 0.6 copy-start.12
  29.0 40.0 %copy-start.16 = (f32[1024]{0:T(1024)}, f32[1024]{0:T(1024)S(1)}, u32[]{:S(2)}) copy-start(f32[1024]{0:T(1024)S(1)} %add_rsqrt_fusion) | copy-start | bytes 12292
  29.7 39.3 %copy-start.6 = (f32[2048]{0:T(1024)}, f32[2048]{0:T(1024)S(1)}, u32[]{:S(2)}) copy-start(f32[2048]{0:T(1024)S(1)} %convert_element_type.81) | copy-start | bytes 24580
  101.7 1484.1 %reduce-scatter.3.cloned.1.call-start = ((), (), s32[]{:S(2)}) async-start(), calls=%async_computation.7 | async-start | bytes 83886080 | tf_op jit(solution)/shard_map/reduce_scatter | solution.py:43
  1033.2 0.7 copy-start.23
  1033.2 6.0 copy-start.10
  1033.2 6.5 copy-start.9
  1033.2 6.5 copy-start.13
  1033.2 1390.1 %all-gather.5.cloned.1.call-start = ((), (), s32[]{:S(2)}) async-start(), calls=%async_computation.8 | async-start | bytes 83886080 | tf_op jit(solution)/shard_map/all_gather | solution.py:40
  1038.5 0.6 copy-start.1
  1039.7 731.2 %copy-start.19 = (pred[2048]{0:T(1024)(128)(4,1)}, pred[2048]{0:T(1024)(128)(4,1)S(1)}, u32[]{:S(2)}) copy-start(pred[2048]{0:T(1024)(128)(4,1)S(1)} %compare_and_fusion.2) | copy-start | bytes 6148
  1039.7 603.9 %copy-start.14 = (s32[2048]{0:T(1024)}, s32[2048]{0:T(1024)S(1)}, u32[]{:S(2)}) copy-start(s32[2048]{0:T(1024)S(1)} %broadcast_clamp_fusion.1) | copy-start | bytes 24580
  1770.9 13.0 copy-start.18
  1784.0 35.8 %copy-start.22 = (pred[2,4,512]{2,1,0:T(4,128)(4,1)S(1)}, pred[2,4,512]{2,1,0:T(4,128)(4,1)}, u32[]{:S(2)}) copy-start(pred[2,4,512]{2,1,0:T(4,128)(4,1)} %broadcast_in_dim.60) | copy-start | bytes 12292
  1852.1 1509.6 %reduce-scatter.5.cloned.1.call-start = ((), (), s32[]{:S(2)}) async-start(), calls=%async_computation.9 | async-start | bytes 83886080 | tf_op jit(solution)/shard_map/reduce_scatter | solution.py:43
  2807.9 0.7 copy-start.21
  2807.9 1.4 copy-start.11
  2807.9 1.5 copy-start.24
  2807.9 25.7 copy-start.2
  2833.7 109.2 %copy-start.4 = (bf16[1024,8]{0,1:T(8,128)(2,1)}, bf16[1024,8]{0,1:T(8,128)(2,1)S(1)}, u32[]{:S(2)}) copy-start(bf16[1024,8]{0,1:T(8,128)(2,1)S(1)} %multiply_convert_fusion.4) | copy-start | bytes 49156
  3398.3 21.1 copy-start.15
  3419.4 24.3 copy-start.20
  3473.9 24.7 copy-start.5
  3473.9 24.7 copy-start.7
  3473.9 24.7 copy-start.17
  3498.6 8.0 copy-start.3
Sparse Core Ops, SparseCore 0:
  101.8 573.5 all-gather.2
  1033.3 552.4 reduce-scatter.2
  1852.2 571.0 all-gather.4
  2808.0 553.6 reduce-scatter.4
where the time goes:
time: 3560 us; the launch traced here: 3550 us
  waiting for transfers between devices  1880 us (53%)
  matrix products  1090 us (31%)
  local copies, waits for them, and re-layouts  291 us (8%)
  other arithmetic  150 us (4%)
  blocking collectives  117 us (3%)
    all_gather x2, waiting for transfers between devices, to_experts(): lax.all_gather(sent.reshape(local_experts, ep_size * capacity, model_dim)...  1140 us
    reduce_scatter x2, waiting for transfers between devices, from_experts(): summed = lax.psum_scatter(part_rows, 'tp', scatter_dimension=1, tiled=True)  735 us
    dot_general x1, matrix products, body(): jnp.einsum('ecd,efd->ecf', rows_grad, w_down, preferred_element_type=jnp....  149 us
    dot_general x1, matrix products, body(): jnp.einsum('ecd,edf->ecf', rows_in, w_up, preferred_element_type=jnp.floa...  129 us
    dot_general x1, matrix products, body(): jnp.einsum('ecf,edf->ecd', pre_up_grad, w_up, preferred_element_type=jnp....  120 us
    dot_general x1, matrix products, body(): jnp.einsum('ecf,edf->ecd', pre_gate_grad, w_gate, preferred_element_type=...  115 us
    dot_general x1, matrix products, body(): jnp.einsum('ecd,edf->ecf', rows_in, w_gate, preferred_element_type=jnp.fl...  115 us
    dot_general x1, matrix products, body(): jnp.einsum('ecd,ecf->edf', rows_in, pre_up_grad, preferred_element_type=j...  115 us
  transfers between devices with their start and end apart: 4, of which 4 were waited for; matrix products, arithmetic and copies ran while one was open for 10% of the time, Pallas kernels for 0%

commit v1 on v0

v1 whole, which is shorter than its diff:
```python
import functools

import jax
import jax.numpy as jnp
from jax import lax
from jax.experimental import pallas as pl
from jax.experimental.pallas import tpu as pltpu
from jax.sharding import PartitionSpec as P

NORM_EPS = 1e-6
ACT_COEF = 1e-5
BALANCE_COEF = 1e-3
TILE = 256
HALF = 128
LANES = 128
CHUNKS = 2
VMEM_LIMIT = 62 * 1024 * 1024


def params(**kwargs):
    return pltpu.CompilerParams(vmem_limit_bytes=VMEM_LIMIT, **kwargs)


def row_block(height, width):
    return pl.BlockSpec((height, width), lambda t: (t, 0))


def dispatch_kernel(with_gate, count_ref, group_ref, lo_ref, steps_ref, pos_ref, prob_ref, tok_hbm, *rest):
    outs = rest[:2 if with_gate else 1]
    scratch = rest[len(outs):]
    specs = [row_block(HALF, out.shape[1]) for out in outs]

    def tile_body(*blocks):
        dispatch_tile(with_gate, group_ref, lo_ref, steps_ref, pos_ref, prob_ref, tok_hbm, *blocks, *scratch)

    pltpu.emit_pipeline(tile_body, grid=(count_ref[0] * (TILE // HALF),), out_specs=specs)(*outs)


def dispatch_tile(with_gate, group_ref, lo_ref, steps_ref, pos_ref, prob_ref, tok_hbm, *rest):
    if with_gate:
        x_ref, gate_ref, tok, acc, waited, sems = rest
    else:
        x_ref, tok, acc, waited, sems = rest
    tile = pl.program_id(0)
    tokens = tok.shape[0]
    blocks = tokens // TILE
    expert = group_ref[tile // (TILE // HALF)]
    lo = lo_ref[tile]
    steps = steps_ref[tile]
    row_id = lax.broadcasted_iota(jnp.int32, (HALF, LANES), 0) + tile * HALF

    def block_copy(index):
        rows = pl.ds(pl.multiple_of(index * TILE, TILE), TILE)
        return pltpu.make_async_copy(tok_hbm.at[rows, :], tok.at[rows, :], sems.at[index])

    @pl.when(tile == 0)
    def _():
        waited[0] = 0

        @pl.loop(0, blocks)
        def _(index):
            block_copy(index).start()

    def await_tokens(stop_chunk):
        need = (stop_chunk * LANES + TILE - 1) // TILE

        @pl.loop(waited[0], need)
        def _(index):
            block_copy(index).wait()

        waited[0] = jnp.maximum(waited[0], need)

    def window(start, count, first=None):
        hot, gate = [], jnp.zeros((HALF, LANES), jnp.float32)
        for q in range(count):
            match = pos_ref[expert, pl.ds(start + q, 1), :] == row_id
            if first is not None:
                match = jnp.logical_and(match, jnp.broadcast_to(start + q >= first, match.shape))
            hot.append(jnp.where(match, 1.0, 0.0).astype(jnp.bfloat16))
            if with_gate:
                gate = gate + jnp.where(match, prob_ref[expert, pl.ds(start + q, 1), :], 0.0)
        rows = tok[pl.ds(pl.multiple_of(start * LANES, LANES), count * LANES), :]
        return jnp.dot(jnp.concatenate(hot, axis=1), rows, preferred_element_type=jnp.float32), gate

    def put_gate(gate):
        if with_gate:
            gate_ref[...] = jnp.broadcast_to(jnp.sum(gate, axis=1, keepdims=True), (HALF, LANES))

    @pl.when(steps == 0)
    def _():
        x_ref[...] = jnp.zeros_like(x_ref)
        put_gate(jnp.zeros((HALF, LANES), jnp.float32))

    for k in range(1, 5):
        @pl.when(steps == k)
        def _(k=k):
            start = jnp.minimum(lo, tokens // LANES - 2 * k)
            await_tokens(start + 2 * k)
            out, gate = window(start, 2 * k)
            x_ref[...] = out.astype(x_ref.dtype)
            put_gate(gate)

    @pl.when(steps > 4)
    def _():
        acc[...] = jnp.zeros_like(acc)
        if with_gate:
            gate_ref[...] = jnp.zeros_like(gate_ref)

        @pl.loop(0, (steps + 3) // 4)
        def _(index):
            first = lo + 8 * index
            start = jnp.minimum(first, tokens // LANES - 8)
            await_tokens(start + 8)
            out, gate = window(start, 8, first)
            acc[...] += out
            if with_gate:
                gate_ref[...] += gate

        x_ref[...] = acc[...].astype(x_ref.dtype)
        if with_gate:
            put_gate(gate_ref[...])

    @pl.when(tile == pl.num_programs(0) - 1)
    def _():
        await_tokens(tokens // LANES)


def dispatch(meta, pos, prob, tok, rows_max, with_gate):
    tokens, dim = tok.shape
    any_spec = pl.BlockSpec(memory_space=pl.ANY)
    whole = pl.BlockSpec(memory_space=pltpu.VMEM)
    out_shape = [jax.ShapeDtypeStruct((rows_max, dim), jnp.bfloat16)]
    if with_gate:
        out_shape.append(jax.ShapeDtypeStruct((rows_max, LANES), jnp.float32))
    return pl.pallas_call(
        functools.partial(dispatch_kernel, with_gate),
        grid_spec=pltpu.PrefetchScalarGridSpec(
            num_scalar_prefetch=4,
            in_specs=[whole, whole, any_spec],
            out_specs=[any_spec] * len(out_shape),
            scratch_shapes=[
                pltpu.VMEM((tokens, dim), jnp.bfloat16),
                pltpu.VMEM((HALF, dim), jnp.float32),
                pltpu.SMEM((1,), jnp.int32),
                pltpu.SemaphoreType.DMA((tokens // TILE,)),
            ],
        ),
        out_shape=out_shape,
        compiler_params=params(),
        cost_estimate=pl.CostEstimate(flops=22 * 10**9, bytes_accessed=45 * 10**6, transcendentals=0),
        name="dispatch",
    )(meta["count"], meta["group"], meta["lo"], meta["steps"], pos, prob, tok)


def combine_kernel(with_gate, local_experts, start_ref, first_ref, over_ref, count_ref, pos_ref, rows_hbm, *rest):
    if with_gate:
        gate_hbm, out_ref, gout_ref, rows, gates, waited, sems = rest
    else:
        out_ref, rows, waited, sems = rest
    tile = pl.program_id(0)
    tiles = pl.num_programs(0)
    row_iota = lax.broadcasted_iota(jnp.int32, (HALF, LANES), 0)
    total_rows = count_ref[0] * TILE

    def block_copies(index):
        at = pl.ds(pl.multiple_of(index * TILE, TILE), TILE)
        copies = [pltpu.make_async_copy(rows_hbm.at[at, :], rows.at[at, :], sems.at[0, index])]
        if with_gate:
            copies.append(pltpu.make_async_copy(gate_hbm.at[at, :], gates.at[at, :], sems.at[1, index]))
        return copies

    @pl.when(tile == 0)
    def _():
        for e in range(local_experts):
            waited[e] = first_ref[e]

        @pl.loop(0, count_ref[0])
        def _(index):
            for copy in block_copies(index):
                copy.start()

    starts = []
    for e in range(local_experts):
        starts.append(pl.multiple_of(start_ref[e * tiles + tile], 16))

    over = over_ref[tile]
    for e in range(local_experts):
        stop = first_ref[e + 1]
        need = jnp.minimum((starts[e] + HALF + over * HALF + TILE - 1) // TILE, stop)

        @pl.loop(waited[e], need)
        def _(index):
            for copy in block_copies(index):
                copy.wait()

        waited[e] = jnp.maximum(waited[e], need)

    def window(second):
        hot, data, gdata = [], [], []
        for e in range(local_experts):
            if second:
                begin = starts[e] + HALF
                at = pl.multiple_of(jnp.minimum(begin, total_rows - HALF), 16)
            else:
                begin = at = starts[e]
            row = row_iota + at
            match = pos_ref[e, pl.ds(tile, 1), :] == row
            if second:
                match = jnp.logical_and(match, row >= begin)
            hot.append(jnp.where(match, 1.0, 0.0).astype(jnp.bfloat16))
            data.append(rows[pl.ds(at, HALF), :])
            if with_gate:
                gdata.append(gates[pl.ds(at, HALF), :])
        hot = jnp.concatenate(hot, axis=0)
        dims = (((0,), (0,)), ((), ()))
        out = lax.dot_general(hot, jnp.concatenate(data, axis=0), dims, preferred_element_type=jnp.float32)
        if not with_gate:
            return out, None
        exact = jnp.concatenate(gdata, axis=0)
        high = exact.astype(jnp.bfloat16)
        low = (exact - high.astype(jnp.float32)).astype(jnp.bfloat16)
        pair = lax.dot_general(hot, jnp.concatenate([high, low], axis=1), dims, preferred_element_type=jnp.float32)
        return out, pair[:, :LANES] + pair[:, LANES:]

    @pl.when(over == 0)
    def _():
        out, gate = window(False)
        out_ref[...] = out.astype(out_ref.dtype)
        if with_gate:
            gout_ref[...] = gate

    @pl.when(over != 0)
    def _():
        out, gate = window(False)
        out2, gate2 = window(True)
        out_ref[...] = (out + out2).astype(out_ref.dtype)
        if with_gate:
            gout_ref[...] = gate + gate2

    @pl.when(tile == tiles - 1)
    def _():
        for e in range(local_experts):
            @pl.loop(waited[e], first_ref[e + 1])
            def _(index):
                for copy in block_copies(index):
                    copy.wait()


def combine(meta, pos, rows, tokens, gate_rows=None):
    rows_max, dim = rows.shape
    local_experts = pos.shape[0]
    with_gate = gate_rows is not None
    any_spec = pl.BlockSpec(memory_space=pl.ANY)
    out_shape = [jax.ShapeDtypeStruct((tokens, dim), jnp.bfloat16)]
    out_specs = [pl.BlockSpec((HALF, dim), lambda t, *_: (t, 0))]
    scratch = [pltpu.VMEM((rows_max, dim), jnp.bfloat16)]
    if with_gate:
        out_shape.append(jax.ShapeDtypeStruct((tokens, LANES), jnp.float32))
        out_specs.append(pl.BlockSpec((HALF, LANES), lambda t, *_: (t, 0)))
        scratch.append(pltpu.VMEM((rows_max, LANES), jnp.float32))
    operands = (rows, gate_rows) if with_gate else (rows,)
    return pl.pallas_call(
        functools.partial(combine_kernel, with_gate, local_experts),
        grid_spec=pltpu.PrefetchScalarGridSpec(
            num_scalar_prefetch=4,
            grid=(tokens // HALF,),
            in_specs=[pl.BlockSpec(pos.shape, lambda t, *_: (0, 0, 0))] + [any_spec] * len(operands),
            out_specs=out_specs,
            scratch_shapes=scratch + [
                pltpu.SMEM((local_experts,), jnp.int32),
                pltpu.SemaphoreType.DMA((2, rows_max // TILE)),
            ],
        ),
        out_shape=out_shape,
        compiler_params=params(),
        cost_estimate=pl.CostEstimate(flops=11 * 10**9, bytes_accessed=40 * 10**6, transcendentals=0),
        name="combine",
    )(meta["start"], meta["first"], meta["over"], meta["count"], pos, *operands)


def weight_stream(group_ref, wg_hbm, wu_hbm, wd_hbm, wide, down, sems):
    tile = pl.program_id(0)
    experts = wg_hbm.shape[0]
    ffn = wg_hbm.shape[2]
    expert = group_ref[tile]
    slot = lax.rem(expert, 2)

    def copies(e, s):
        return (
            pltpu.make_async_copy(wg_hbm.at[e], wide.at[s, :, pl.ds(0, ffn)], sems.at[s, 0]),
            pltpu.make_async_copy(wu_hbm.at[e], wide.at[s, :, pl.ds(ffn, ffn)], sems.at[s, 1]),
            pltpu.make_async_copy(wd_hbm.at[e], down.at[s], sems.at[s, 2]),
        )

    @pl.when(tile == 0)
    def _():
        for copy in copies(0, 0):
            copy.start()

    fresh = jnp.logical_or(tile == 0, expert != group_ref[jnp.maximum(tile - 1, 0)])

    @pl.when(fresh)
    def _():
        @pl.when(expert + 1 < experts)
        def _():
            for copy in copies(expert + 1, 1 - slot):
                copy.start()

        for copy in copies(expert, slot):
            copy.wait()

    return slot


def forward_kernel(count_ref, group_ref, x_hbm, gate_hbm, wg_hbm, wu_hbm, wd_hbm, ab_hbm, h_hbm, out_hbm, wide, down, sems):
    def tile_body(x_ref, gate_ref, *outs):
        forward_tile(group_ref, x_ref, gate_ref, wg_hbm, wu_hbm, wd_hbm, *outs, wide, down, sems)

    piped_in, piped_out = (x_hbm, gate_hbm), (ab_hbm, h_hbm, out_hbm)
    pipeline = pltpu.emit_pipeline(
        tile_body, grid=(count_ref[0],),
        in_specs=[row_block(TILE, ref.shape[1]) for ref in piped_in],
        out_specs=[row_block(TILE, ref.shape[1]) for ref in piped_out],
    )
    pipeline(*piped_in, *piped_out)


def forward_tile(group_ref, x_ref, gate_ref, wg_hbm, wu_hbm, wd_hbm, ab_ref, h_ref, out_ref, wide, down, sems):
    slot = weight_stream(group_ref, wg_hbm, wu_hbm, wd_hbm, wide, down, sems)
    ffn = wg_hbm.shape[2]
    x = x_ref[...]
    for j in range(ffn // LANES):
        cols = slice(j * LANES, (j + 1) * LANES)
        ucols = slice(ffn + j * LANES, ffn + (j + 1) * LANES)
        weights = jnp.concatenate([wide[slot, :, cols], wide[slot, :, ucols]], axis=1)
        both = jnp.dot(x, weights, preferred_element_type=jnp.float32)
        a, b = both[:, :LANES], both[:, LANES:]
        ab_ref[:, cols] = a
        ab_ref[:, ucols] = b
        h_ref[:, cols] = (a * jax.nn.sigmoid(a) * b).astype(h_ref.dtype)
    out = jnp.dot(h_ref[...], down[slot], preferred_element_type=jnp.float32)
    gate = gate_ref[...]
    for j in range(out.shape[1] // LANES):
        cols = slice(j * LANES, (j + 1) * LANES)
        out_ref[:, cols] = (out[:, cols] * gate).astype(out_ref.dtype)


def backward_kernel(count_ref, group_ref, base_ref, m_hbm, ab_hbm, h_hbm, gate_hbm, wg_hbm, wu_hbm, wd_hbm, *rest):
    piped_in, piped_out, weights = (m_hbm, ab_hbm, h_hbm, gate_hbm), rest[:4], (wg_hbm, wu_hbm, wd_hbm)

    def tile_body(*blocks):
        backward_tile(group_ref, base_ref, *blocks[:4], *weights, *blocks[4:], *rest[4:])

    pipeline = pltpu.emit_pipeline(
        tile_body, grid=(count_ref[0],),
        in_specs=[row_block(TILE, ref.shape[1]) for ref in piped_in],
        out_specs=[row_block(TILE, ref.shape[1]) for ref in piped_out],
    )
    pipeline(*piped_in, *piped_out)


def backward_tile(group_ref, base_ref, m_ref, ab_ref, h_ref, gate_ref, wg_hbm, wu_hbm, wd_hbm, d_ref, in_ref, mg_ref, dgate_ref, wide, down, sems):
    slot = weight_stream(group_ref, wg_hbm, wu_hbm, wd_hbm, wide, down, sems)
    ffn = wg_hbm.shape[2]
    trans = (((1,), (1,)), ((), ()))
    m = m_ref[...]
    gate = gate_ref[...]
    dgate = jnp.zeros(gate.shape, jnp.float32)
    for c in range(0, ffn, 2 * LANES):
        width = min(2 * LANES, ffn - c)
        raw = lax.dot_general(m, down[slot, c:c + width, :], trans, preferred_element_type=jnp.float32)
        for k in range(width // LANES):
            lo = c + k * LANES
            cols = slice(lo, lo + LANES)
            ucols = slice(ffn + lo, ffn + lo + LANES)
            g = raw[:, k * LANES:(k + 1) * LANES]
            a, b = ab_ref[:, cols], ab_ref[:, ucols]
            sig = jax.nn.sigmoid(a)
            hidden_grad = g * gate
            d_ref[:, cols] = (hidden_grad * b * sig * (1.0 + a * (1.0 - sig))).astype(d_ref.dtype)
            d_ref[:, ucols] = (hidden_grad * (a * sig)).astype(d_ref.dtype)
            dgate = dgate + g * h_ref[:, cols].astype(jnp.float32)
    in_ref[...] = lax.dot_general(d_ref[...], wide[slot], trans, preferred_element_type=jnp.float32).astype(in_ref.dtype)
    for j in range(m.shape[1] // LANES):
        cols = slice(j * LANES, (j + 1) * LANES)
        mg_ref[:, cols] = (m[:, cols].astype(jnp.float32) * gate).astype(mg_ref.dtype)
    lane = lax.broadcasted_iota(jnp.int32, gate.shape, 1)
    mine = base_ref[0] + group_ref[pl.program_id(0)]
    dgate_ref[...] = jnp.where(lane == mine, jnp.sum(dgate, axis=1, keepdims=True), 0.0)


def weight_scratch(wg):
    _, dim, ffn = wg.shape
    return [
        pltpu.VMEM((2, dim, 2 * ffn), wg.dtype),
        pltpu.VMEM((2, ffn, dim), wg.dtype),
        pltpu.SemaphoreType.DMA((2, 3)),
    ]


def forward(meta, x_rows, gate_rows, wg, wu, wd):
    rows_max, dim = x_rows.shape
    ffn = wg.shape[2]
    any_spec = pl.BlockSpec(memory_space=pl.ANY)
    return pl.pallas_call(
        forward_kernel,
        grid_spec=pltpu.PrefetchScalarGridSpec(
            num_scalar_prefetch=2,
            in_specs=[any_spec] * 5,
            out_specs=[any_spec] * 3,
            scratch_shapes=weight_scratch(wg),
        ),
        out_shape=[
            jax.ShapeDtypeStruct((rows_max, 2 * ffn), jnp.float32),
            jax.ShapeDtypeStruct((rows_max, ffn), jnp.bfloat16),
            jax.ShapeDtypeStruct((rows_max, dim), jnp.bfloat16),
        ],
        compiler_params=params(),
        cost_estimate=pl.CostEstimate(flops=95 * 10**9, bytes_accessed=190 * 10**6, transcendentals=0),
        name="forward",
    )(meta["count"], meta["group"], x_rows, gate_rows, wg, wu, wd)


def backward(meta, base, m_rows, ab, hidden, gate_rows, wg, wu, wd):
    rows_max, dim = m_rows.shape
    ffn = wg.shape[2]
    any_spec = pl.BlockSpec(memory_space=pl.ANY)
    return pl.pallas_call(
        backward_kernel,
        grid_spec=pltpu.PrefetchScalarGridSpec(
            num_scalar_prefetch=3,
            in_specs=[any_spec] * 7,
            out_specs=[any_spec] * 4,
            scratch_shapes=weight_scratch(wg),
        ),
        out_shape=[
            jax.ShapeDtypeStruct((rows_max, 2 * ffn), jnp.bfloat16),
            jax.ShapeDtypeStruct((rows_max, dim), jnp.bfloat16),
            jax.ShapeDtypeStruct((rows_max, dim), jnp.bfloat16),
            jax.ShapeDtypeStruct((rows_max, LANES), jnp.float32),
        ],
        compiler_params=params(),
        cost_estimate=pl.CostEstimate(flops=95 * 10**9, bytes_accessed=220 * 10**6, transcendentals=0),
        name="backward",
    )(meta["count"], meta["group"], base, m_rows, ab, hidden, gate_rows, wg, wu, wd)


def weight_grad_kernel(tiles_max, outs, begin_ref, src0_ref, src1_ref, pair_ref, la_hbm, lb_hbm, ra_hbm, rb_hbm, *rest):
    out_refs, (lhs, rhs, lhs_t, acc, sems) = rest[:outs], rest[outs:]
    expert = pl.program_id(0)
    experts = pl.num_programs(0)
    begin, stop, steps = begin_ref[expert], begin_ref[expert + 1], begin_ref[experts]

    def copies(chunk, row, s, half):
        src_l, src_r = ((la_hbm, ra_hbm), (lb_hbm, rb_hbm))[chunk]
        at = pl.ds(pl.multiple_of(row, TILE), TILE)
        into = pl.ds(half * TILE, TILE)
        return (
            pltpu.make_async_copy(src_l.at[at, :], lhs.at[s, into, :], sems.at[s, half, 0]),
            pltpu.make_async_copy(src_r.at[at, :], rhs.at[s, into, :], sems.at[s, half, 1]),
        )

    def start_half(src, s, half):
        @pl.when(src < tiles_max)
        def _():
            for copy in copies(0, src * TILE, s, half):
                copy.start()

        @pl.when(src >= tiles_max)
        def _():
            for copy in copies(1, (src - tiles_max) * TILE, s, half):
                copy.start()

    def start(index, s):
        start_half(src0_ref[index], s, 0)

        @pl.when(pair_ref[index] != 0)
        def _():
            start_half(src1_ref[index], s, 1)

    @pl.when(expert == 0)
    def _():
        start(0, 0)

    def accumulate(slot, fresh, depth):
        lhs_t[:, :depth] = jnp.transpose(lhs[slot, :depth, :], (1, 0))
        block = 2 * LANES
        for c in range(0, acc.shape[1], block):
            part = jnp.dot(lhs_t[:, :depth], rhs[slot, :depth, c:c + block], preferred_element_type=jnp.float32)
            acc[:, c:c + block] = jnp.where(fresh, 0.0, acc[:, c:c + block]) + part

    @pl.loop(begin, stop)
    def _(step):
        slot = lax.rem(step, 2)

        @pl.when(step + 1 < steps)
        def _():
            start(step + 1, 1 - slot)

        fresh = step == begin
        pair = pair_ref[step] != 0
        for copy in copies(0, 0, slot, 0):
            copy.wait()

        @pl.when(pair)
        def _():
            for copy in copies(0, 0, slot, 1):
                copy.wait()
            accumulate(slot, fresh, 2 * TILE)

        @pl.when(jnp.logical_not(pair))
        def _():
            accumulate(slot, fresh, TILE)

    width = acc.shape[1] // outs
    for i in range(outs):
        out_refs[i][...] = acc[:, i * width:(i + 1) * width].astype(out_refs[i].dtype)


def weight_grad(meta, lhs, rhs, experts, outs, tiles_max):
    rows_max, left = lhs[0].shape
    right = rhs[0].shape[1]
    width = right // outs
    any_spec = pl.BlockSpec(memory_space=pl.ANY)
    return pl.pallas_call(
        functools.partial(weight_grad_kernel, tiles_max, outs),
        grid_spec=pltpu.PrefetchScalarGridSpec(
            num_scalar_prefetch=4,
            grid=(experts,),
            in_specs=[any_spec] * 4,
            out_specs=[pl.BlockSpec((pl.squeezed, left, width), lambda e, *_: (e, 0, 0))] * outs,
            scratch_shapes=[
                pltpu.VMEM((2, 2 * TILE, left), jnp.bfloat16),
                pltpu.VMEM((2, 2 * TILE, right), jnp.bfloat16),
                pltpu.VMEM((left, 2 * TILE), jnp.bfloat16),
                pltpu.VMEM((left, right), jnp.float32),
                pltpu.SemaphoreType.DMA((2, 2, 2)),
            ],
        ),
        out_shape=[jax.ShapeDtypeStruct((experts, left, width), jnp.bfloat16)] * outs,
        compiler_params=params(),
        cost_estimate=pl.CostEstimate(flops=2 * 10000 * left * right, bytes_accessed=100 * 10**6, transcendentals=0),
        name="weight_grad",
    )(meta["begin"], meta["src0"], meta["src1"], meta["pair"], *lhs, *rhs)


def below(size, strict):
    i = lax.broadcasted_iota(jnp.int32, (size, size), 0)
    j = lax.broadcasted_iota(jnp.int32, (size, size), 1)
    return (i < j if strict else i <= j).astype(jnp.float32)


def running(values):
    size = values.shape[0]
    i = lax.broadcasted_iota(jnp.int32, (size, size), 0)
    j = lax.broadcasted_iota(jnp.int32, (size, size), 1)
    return jnp.sum(jnp.where(i <= j, values[:, None], 0), axis=0)


def routing(hot, tiles_max):
    experts, tokens = hot.shape
    spans = tokens // LANES
    hot = hot.reshape(experts, spans, LANES)
    within = jnp.einsum("esi,ij->esj", hot, below(LANES, False), preferred_element_type=jnp.float32)
    span_count = jnp.sum(hot, axis=-1)
    before = jnp.einsum("ei,ij->ej", span_count, below(spans, True), preferred_element_type=jnp.float32)
    total = jnp.sum(span_count, axis=-1).astype(jnp.int32)
    tiles = jnp.maximum((total + TILE - 1) // TILE, 1)
    tile_stop = running(tiles)
    tile_start = tile_stop - tiles
    base = tile_start * TILE
    span_first = base[:, None] + before.astype(jnp.int32)
    span_stop = span_first + span_count.astype(jnp.int32)
    pos = jnp.where(hot > 0, span_first[:, :, None] + within.astype(jnp.int32) - 1, -1)
    count = tile_stop[experts - 1]

    tile_iota = jnp.arange(tiles_max, dtype=jnp.int32)
    group = jnp.sum((tile_iota[:, None] >= tile_stop[None, :experts - 1]).astype(jnp.int32), axis=1)
    halves = tiles_max * (TILE // HALF)
    half_iota = jnp.arange(halves, dtype=jnp.int32)
    half_group = jnp.sum((half_iota[:, None] // (TILE // HALF) >= tile_stop[None, :experts - 1]).astype(jnp.int32), axis=1)
    pick = half_group[:, None] == jnp.arange(experts, dtype=jnp.int32)[None, :]
    stops = jnp.sum(jnp.where(pick[:, :, None], span_stop[None], 0), axis=1)
    row0 = half_iota[:, None] * HALF
    lo = jnp.sum((stops <= row0).astype(jnp.int32), axis=1)
    hi = jnp.minimum(jnp.sum((stops < row0 + HALF).astype(jnp.int32), axis=1), spans - 1)
    steps = (hi - lo + 2) // 2
    start = jnp.minimum(span_first // 16 * 16, count * TILE - HALF)
    over = jnp.any(span_stop - start > HALF, axis=0).astype(jnp.int32)
    first = jnp.concatenate([jnp.zeros((1,), jnp.int32), tile_stop])
    return pos, tile_start, tiles, {
        "group": group, "lo": lo, "steps": steps,
        "start": start.reshape(-1), "first": first, "over": over, "count": count.reshape(1),
    }


def pair_tables(starts, tiles, tiles_max):
    experts = tiles[0].shape[0]
    both = tiles[0] + tiles[1]
    stop = running((both + 1) // 2)
    begin = stop - (both + 1) // 2
    step = jnp.arange(tiles_max + experts, dtype=jnp.int32)
    expert = jnp.sum((step[:, None] >= stop[None, :experts - 1]).astype(jnp.int32), axis=1)
    pick = expert[:, None] == jnp.arange(experts, dtype=jnp.int32)[None, :]

    def of(table):
        return jnp.sum(jnp.where(pick, table[None, :], 0), axis=1)

    first = 2 * (step - of(begin))
    in_a = of(tiles[0])

    def source(index):
        return jnp.where(index < in_a, of(starts[0]) + index, tiles_max + of(starts[1]) + index - in_a)

    pair = (first + 1 < of(both)).astype(jnp.int32)
    return {
        "begin": jnp.concatenate([jnp.zeros((1,), jnp.int32), stop]), "src0": source(first),
        "src1": jnp.where(pair != 0, source(first + 1), 0), "pair": pair,
    }


def solution(mesh):
    tp_size = mesh.shape["tp"]
    ep_size = mesh.shape["ep"]
    dev_count = tp_size * ep_size
    rows_axes = ("ep", "tp")
    row_spec = P(rows_axes, None)
    wide_spec = P("ep", None, "tp")
    down_spec = P("ep", "tp", None)

    def body(x, y_grad, expert_ids, norm_gain, w_router, w_gate, w_up, w_down):
        tokens, model_dim = x.shape
        top_k = expert_ids.shape[1]
        num_experts = w_router.shape[1]
        local_experts = w_gate.shape[0]
        total_tokens = tokens * dev_count
        part = tokens // CHUNKS
        chunk_tokens = part * dev_count
        tiles_max = chunk_tokens * top_k // TILE + local_experts
        rows_max = tiles_max * TILE
        my_base = lax.axis_index("ep") * local_experts

        x_float = x.astype(jnp.float32)
        inv_rms = lax.rsqrt(jnp.mean(x_float * x_float, axis=-1, keepdims=True) + NORM_EPS)
        unit = x_float * inv_rms
        gain = norm_gain.astype(jnp.float32)
        x_norm = (unit * gain).astype(jnp.bfloat16)

        def gather(rows):
            return lax.all_gather(rows, rows_axes, axis=0, tiled=True)

        def scatter(rows):
            return lax.psum_scatter(rows, rows_axes, scatter_dimension=0, tiled=True)

        def of_chunk(rows, c):
            return rows[c * part:(c + 1) * part]

        tok = [gather(of_chunk(x_norm, c)) for c in range(CHUNKS)]

        route_prob = jax.nn.softmax(jnp.dot(x_norm, w_router, preferred_element_type=jnp.float32), axis=-1)
        expert_range = jnp.arange(num_experts, dtype=jnp.int32)
        choice = jnp.sum((expert_ids[:, :, None] == expert_range[None, None, :]).astype(jnp.float32), axis=1)
        small = lax.all_gather(jnp.concatenate([choice, route_prob], axis=1).T, rows_axes, axis=0, tiled=False)
        all_choice, all_prob = small[:, :num_experts], small[:, num_experts:]
        counts = jnp.sum(all_choice, axis=(0, 2))
        balance_scale = BALANCE_COEF * num_experts / (total_tokens * total_tokens * top_k)
        balance_loss = balance_scale * jnp.sum(counts * jnp.sum(all_prob, axis=(0, 2)))

        def mine(values, c):
            own = lax.dynamic_slice_in_dim(values, my_base, local_experts, axis=1)
            own = own[:, :, c * part:(c + 1) * part]
            return own.transpose(1, 0, 2).reshape(local_experts, chunk_tokens)

        pos, prob, meta, starts, tiles = [], [], [], [], []
        for c in range(CHUNKS):
            p, s, t, m = routing(mine(all_choice, c), tiles_max)
            pos.append(p)
            starts.append(s)
            tiles.append(t)
            meta.append(m)
            prob.append(mine(all_prob, c).reshape(p.shape))

        x_rows, gate_rows, pre, hidden, moe_out, m_tok = [], [], [], [], [], []
        grad_scale = 2.0 * ACT_COEF / (total_tokens * model_dim)

        def out_cotangent(c):
            moe_grad = of_chunk(y_grad, c).astype(jnp.float32) + grad_scale * moe_out[c]
            return moe_grad.astype(jnp.bfloat16)

        raw_out = []
        for c in range(CHUNKS):
            rows, gates = dispatch(meta[c], pos[c], prob[c], tok[c], rows_max, True)
            ab, h, out_rows = forward(meta[c], rows, gates, w_gate, w_up, w_down)
            if c > 0:
                out_rows, raw_out[c - 1] = lax.optimization_barrier((out_rows, raw_out[c - 1]))
                moe_out.append(raw_out[c - 1].astype(jnp.float32))
                m_tok.append(gather(out_cotangent(c - 1)))
            (partial,) = combine(meta[c], pos[c], out_rows, chunk_tokens)
            if c > 0:
                partial, m_tok[c - 1] = lax.optimization_barrier((partial, m_tok[c - 1]))
            raw_out.append(scatter(partial))
            x_rows.append(rows)
            gate_rows.append(gates)
            pre.append(ab)
            hidden.append(h)

        base = jnp.reshape(my_base, (1,)).astype(jnp.int32)
        d_rows, mg_rows, returned, gate_part = [], [], [], []
        for c in range(CHUNKS):
            (m_rows,) = dispatch(meta[c], pos[c], prob[c], m_tok[c], rows_max, False)
            d, in_rows, mg, dgate = backward(meta[c], base, m_rows, pre[c], hidden[c], gate_rows[c], w_gate, w_up, w_down)
            if c == 0:
                in_rows, raw_out[-1] = lax.optimization_barrier((in_rows, raw_out[-1]))
                moe_out.append(raw_out[-1].astype(jnp.float32))
                m_tok.append(gather(out_cotangent(CHUNKS - 1)))
            partial, gate_tok = combine(meta[c], pos[c], in_rows, chunk_tokens, dgate)
            if c == 0:
                partial, m_tok[-1] = lax.optimization_barrier((partial, m_tok[-1]))
            returned.append(scatter(partial))
            gate_part.append(gate_tok[:, :num_experts])
            d_rows.append(d)
            mg_rows.append(mg)

        steps = pair_tables(starts, tiles, tiles_max)
        gate_grad, up_grad = weight_grad(steps, x_rows, d_rows, local_experts, 2, tiles_max)
        (down_grad,) = weight_grad(steps, hidden, mg_rows, local_experts, 1, tiles_max)

        moe_all = jnp.concatenate(moe_out, axis=0)
        y = (x_float + moe_all).astype(jnp.bfloat16)
        gate_sum = scatter(jnp.concatenate(gate_part, axis=1))
        gate_weight_grad = jnp.concatenate([gate_sum[:, :num_experts], gate_sum[:, num_experts:]], axis=0)
        prob_grad = gate_weight_grad + balance_scale * counts[None, :]
        logit_grad = (route_prob * (prob_grad - jnp.sum(route_prob * prob_grad, axis=-1, keepdims=True))).astype(jnp.bfloat16)
        x_norm_grad = jnp.concatenate(returned, axis=0).astype(jnp.float32)
        x_norm_grad = x_norm_grad + jnp.einsum("se,de->sd", logit_grad, w_router, preferred_element_type=jnp.float32)
        unit_grad = x_norm_grad * gain
        x_grad = y_grad.astype(jnp.float32) + inv_rms * (unit_grad - unit * jnp.mean(unit_grad * unit, axis=-1, keepdims=True))
        gain_sum, router_sum, act_sum = lax.psum(
            (
                jnp.sum(x_norm_grad * unit, axis=0),
                jnp.einsum("sd,se->de", x_norm, logit_grad, preferred_element_type=jnp.float32),
                jnp.sum(moe_all * moe_all),
            ),
            ("tp", "ep"),
        )
        act_loss = ACT_COEF * act_sum / (total_tokens * model_dim)
        return (y, x_grad.astype(jnp.bfloat16), gain_sum.astype(jnp.bfloat16), router_sum.astype(jnp.bfloat16), gate_grad, up_grad, down_grad, balance_loss, act_loss)

    return jax.shard_map(body, mesh=mesh, in_specs=(row_spec, row_spec, row_spec, P(), P(), wide_spec, wide_spec, down_spec), out_specs=(row_spec, row_spec, P(), P(), wide_spec, wide_spec, down_spec, P(), P()), check_vma=False)
```

time: 3560 us -> 1290 us (0.36)
  waiting for transfers between devices: 1880 us -> 162 us
  matrix products: 1090 us -> 17.1 us
  Pallas kernels: 0 us -> 974 us
  local copies, waits for them, and re-layouts: 291 us -> 16 us
  other arithmetic: 150 us -> 46.4 us
  blocking collectives: 117 us -> 42.2 us
    dot_general x9 -> x4, matrix products: 1080 us -> 2.84 us  [the longest x2 1.54 us: routing(): jnp.einsum('esi,ij->esj', hot, below(LANES, False), preferred_element_typ...]
    all_gather x2 -> x4, waiting for transfers between devices: 1140 us -> 158 us  [gather(): return lax.all_gather(rows, rows_axes, axis=0, tiled=True)]
    pallas_call x0 -> x14, Pallas kernels: none -> 974 us  [the longest x2 241 us: forward(): pl.pallas_call(forward_kernel, grid_spec=pltpu.PrefetchScalarGridSpec(num...]
    reduce_scatter x2 -> x5, waiting for transfers between devices: 735 us -> 2.48 us  [scatter(): return lax.psum_scatter(rows, rows_axes, scatter_dimension=0, tiled=True)]
    gather x4 -> x0, local copies, waits for them, and re-layouts: 118 us -> none  [the longest x1 35.8 us: body(): jnp.take(picked_grad, assign_of_slot, axis=0, mode='fill', fill_value=0)]
    all_to_all x4 -> x0, blocking collectives: 70.3 us -> none  [the longest x2 35.3 us: from_experts(): lax.all_to_all(summed.reshape(1, local_experts, ep_size * capacity, model...]
    reduce_sum x9 -> x17, other arithmetic: 79.1 us -> 15.8 us  [the longest x1 11.8 us: body(): jnp.sum(moe_all * moe_all)]
    all_to_all x4 -> x0, local copies, waits for them, and re-layouts: 55.2 us -> none  [the longest x2 42.1 us: from_experts(): lax.all_to_all(summed.reshape(1, local_experts, ep_size * capacity, model...]
  transfers between devices with their start and end apart: 4 -> 9, of which waited for: 4 -> 4; matrix products, arithmetic and copies ran while one was open for 10% -> 3% of each run, Pallas kernels for 0% -> 62%
where the time goes in v1:
time: 1290 us; the launch traced here: 1280 us
  Pallas kernels  974 us (76%)
  waiting for transfers between devices  162 us (13%)
  other arithmetic  46.4 us (4%)
  blocking collectives  42.2 us (3%)
  between operations  19.7 us (2%)
  matrix products  17.1 us (1%)
  local copies, waits for them, and re-layouts  16 us (1%)
    pallas_call x2, Pallas kernels, forward(): pl.pallas_call(forward_kernel, grid_spec=pltpu.PrefetchScalarGridSpec(num...  241 us
    pallas_call x2, Pallas kernels, backward(): pl.pallas_call(backward_kernel, grid_spec=pltpu.PrefetchScalarGridSpec(nu...  240 us
    pallas_call x2, Pallas kernels, weight_grad(): pl.pallas_call(functools.partial(weight_grad_kernel, tiles_max, outs), gr...  228 us
    all_gather x4, waiting for transfers between devices, gather(): return lax.all_gather(rows, rows_axes, axis=0, tiled=True)  158 us
    pallas_call x4, Pallas kernels, dispatch(): pl.pallas_call(functools.partial(dispatch_kernel, with_gate), grid_spec=p...  141 us
    pallas_call x4, Pallas kernels, combine(): pl.pallas_call(functools.partial(combine_kernel, with_gate, local_experts...  123 us
  transfers between devices with their start and end apart: 9, of which 4 were waited for; matrix products, arithmetic and copies ran while one was open for 3% of the time, Pallas kernels for 62%

profile of v1, /device:TPU:0, one launch (start us, length us, event | category | flops | bytes accessed | tf_op | source)
XLA Modules:
  0.0 1278.1 jit_solution(17812864473133897149)
XLA Ops:
  7.2 3.1 fusion.11
  11.0 3.2 fusion.4
  16.3 2.5 fusion.42
  19.7 3.4 fusion.44
  23.7 18.5 %all-gather = f32[128,1024]{1,0:T(8,128)S(1)} all-gather(f32[16,1024]{1,0:T(8,128)S(1)} %maximum_bitcast_fusion), channel_id=2, replica_groups=mesh['tp'=4,'ep'=2] {'ep','tp'}, dimensions={0}, use_global_device_ids=true | all-gather | bytes 589824 | tf_op jit(solution)/shard_map/all_gather | solution.py:663
  53.7 55.0 %all-gather.8.cloned.1.call-done.tok_hbm = bf16[4096,2048]{1,0:T(8,128)(2,1)} async-done(((bf16[512,2048]{1,0:T(8,128)(2,1)}), bf16[4096,2048]{1,0:T(8,128)(2,1)}) %all-gather.8.cloned.1.call-update) | async-done | bytes 16777232 | tf_op jit(solution)/shard_map/all_gather | solution.py:650
  108.8 36.3 %dispatch.5 = (bf16[9216,2048]{1,0:T(8,128)(2,1)}, f32[9216,128]{1,0:T(8,128)}) custom-call(s32[1]{0:T(128)} %slice.67.count_ref, s32[36]{0:T(128)} %convert_reduce_fusion.7.group_ref, s32[72]{0:T(128)} %copy-done.27, s32[72]{0:T(128)} %and_select_fusion.1.steps_ref, s32[4,32,128]{2,1,0:T(8,128)} %fusion.15.pos_ref, f32[4,32,128]{2,1,0:T(8,128)} %reshape_reshape.15.prob_ref, ...), custom_call_target="tpu_custom_call" | custom-call | flops 22000001024 | bytes 45000000 | tf_op jit(solution)/shard_map/dispatch/pallas_call | solution.py:135
  145.0 123.4 %forward.3 = (f32[9216,2816]{1,0:T(8,128)}, bf16[9216,1408]{1,0:T(8,128)(2,1)}, bf16[9216,2048]{1,0:T(8,128)(2,1)}) custom-call(s32[1]{0:T(128)} %slice.67.count_ref, s32[36]{0:T(128)} %convert_reduce_fusion.7.group_ref, bf16[9216,2048]{1,0:T(8,128)(2,1)} %get-tuple-element.44.x_hbm.la_hbm, f32[9216,128]{1,0:T(8,128)} %get-tuple-element.45.gate_hbm, ...), custom_call_target="tpu_custom_call" | custom-call | flops 95000002560 | bytes 190000000 | tf_op jit(solution)/shard_map/forward/pallas_call | solution.py:405
  268.4 30.2 %combine.4 = bf16[4096,2048]{1,0:T(8,128)(2,1)} custom-call(s32[128]{0:T(128)} %reshape.300.start_ref, s32[5]{0:T(128)} %pad_add_fusion.2.first_ref, s32[32]{0:T(128)} %convert_element_type.173.over_ref, s32[1]{0:T(128)} %slice.67.count_ref, s32[4,32,128]{2,1,0:T(8,128)} %fusion.15.pos_ref, bf16[9216,2048]{1,0:T(8,128)(2,1)} %get-tuple-element.46.rows_hbm), custom_call_target="tpu_custom_call" | custom-call | flops 11000000512 | bytes 40000000 | tf_op jit(solution)/shard_map/combine/pallas_call | solution.py:262
  301.4 34.9 %dispatch.4 = (bf16[9216,2048]{1,0:T(8,128)(2,1)}, f32[9216,128]{1,0:T(8,128)}) custom-call(s32[1]{0:T(128)} %slice.61.count_ref, s32[36]{0:T(128)} %convert_reduce_fusion.9.group_ref, s32[72]{0:T(128)} %copy-done.26, s32[72]{0:T(128)} %and_select_fusion.3.steps_ref, s32[4,32,128]{2,1,0:T(8,128)} %fusion.18.pos_ref, f32[4,32,128]{2,1,0:T(8,128)} %reshape_reshape.13.prob_ref, ...), custom_call_target="tpu_custom_call" | custom-call | flops 22000001024 | bytes 45000000 | tf_op jit(solution)/shard_map/dispatch/pallas_call | solution.py:135
  336.3 117.8 %forward.2 = (f32[9216,2816]{1,0:T(8,128)}, bf16[9216,1408]{1,0:T(8,128)(2,1)}, bf16[9216,2048]{1,0:T(8,128)(2,1)}) custom-call(s32[1]{0:T(128)} %slice.61.count_ref, s32[36]{0:T(128)} %convert_reduce_fusion.9.group_ref, bf16[9216,2048]{1,0:T(8,128)(2,1)} %get-tuple-element.41.x_hbm.lb_hbm, f32[9216,128]{1,0:T(8,128)} %get-tuple-element.42.gate_hbm, ...), custom_call_target="tpu_custom_call" | custom-call | flops 95000002560 | bytes 190000000 | tf_op jit(solution)/shard_map/forward/pallas_call | solution.py:405
  454.1 4.5 add_convert_fusion.1
  460.4 29.7 %combine.5 = bf16[4096,2048]{1,0:T(8,128)(2,1)} custom-call(s32[128]{0:T(128)} %reshape.302.start_ref, s32[5]{0:T(128)} %pad_add_fusion.1.first_ref, s32[32]{0:T(128)} %convert_element_type.180.over_ref, s32[1]{0:T(128)} %slice.61.count_ref, s32[4,32,128]{2,1,0:T(8,128)} %fusion.18.pos_ref, bf16[9216,2048]{1,0:T(8,128)(2,1)} %get-tuple-element.48.rows_hbm), custom_call_target="tpu_custom_call" | custom-call | flops 11000000512 | bytes 40000000 | tf_op jit(solution)/shard_map/combine/pallas_call | solution.py:262
  490.2 52.7 %all-gather.10.cloned.1.call-done.tok_hbm = bf16[4096,2048]{1,0:T(8,128)(2,1)} async-done(((bf16[512,2048]{1,0:T(8,128)(2,1)}), bf16[4096,2048]{1,0:T(8,128)(2,1)}) %all-gather.10.cloned.1.call-update) | async-done | bytes 16777232 | tf_op jit(solution)/shard_map/all_gather | solution.py:650
  543.0 36.1 %dispatch.6.m_hbm = bf16[9216,2048]{1,0:T(8,128)(2,1)} custom-call(s32[1]{0:T(128)} %slice.67.count_ref, s32[36]{0:T(128)} %convert_reduce_fusion.7.group_ref, s32[72]{0:T(128)} %copy-done.27, s32[72]{0:T(128)} %and_select_fusion.1.steps_ref, s32[4,32,128]{2,1,0:T(8,128)} %fusion.15.pos_ref, f32[4,32,128]{2,1,0:T(8,128)} %reshape_reshape.15.prob_ref, ...), custom_call_target="tpu_custom_call" | custom-call | flops 22000001024 | bytes 45000000 | tf_op jit(solution)/shard_map/dispatch/pallas_call | solution.py:135
  579.1 122.4 %backward.2 = (bf16[9216,2816]{1,0:T(8,128)(2,1)}, bf16[9216,2048]{1,0:T(8,128)(2,1)}, bf16[9216,2048]{1,0:T(8,128)(2,1)}, f32[9216,128]{1,0:T(8,128)}) custom-call(s32[1]{0:T(128)} %slice.67.count_ref, s32[36]{0:T(128)} %convert_reduce_fusion.7.group_ref, s32[1]{0:T(128)} %bitcast.8.base_ref, bf16[9216,2048]{1,0:T(8,128)(2,1)} %dispatch.6.m_hbm, ...), custom_call_target="tpu_custom_call" | custom-call | flops 95000002560 | bytes 220000000 | tf_op jit(solution)/shard_map/backward/pallas_call | solution.py:428
  701.5 4.5 add_convert_fusion
  706.1 32.0 %combine.6 = (bf16[4096,2048]{1,0:T(8,128)(2,1)}, f32[4096,128]{1,0:T(8,128)}) custom-call(s32[128]{0:T(128)} %reshape.300.start_ref, s32[5]{0:T(128)} %pad_add_fusion.2.first_ref, s32[32]{0:T(128)} %convert_element_type.173.over_ref, s32[1]{0:T(128)} %slice.67.count_ref, s32[4,32,128]{2,1,0:T(8,128)} %fusion.15.pos_ref, ...), custom_call_target="tpu_custom_call" | custom-call | flops 11000000512 | bytes 40000000 | tf_op jit(solution)/shard_map/combine/pallas_call | solution.py:262
  738.1 2.2 copy.40
  740.2 50.0 %all-gather.12.cloned.1.call-done.tok_hbm = bf16[4096,2048]{1,0:T(8,128)(2,1)} async-done(((bf16[512,2048]{1,0:T(8,128)(2,1)}), bf16[4096,2048]{1,0:T(8,128)(2,1)}) %all-gather.12.cloned.1.call-update) | async-done | bytes 16777232 | tf_op jit(solution)/shard_map/all_gather | solution.py:650
  790.3 34.0 %dispatch.7.m_hbm = bf16[9216,2048]{1,0:T(8,128)(2,1)} custom-call(s32[1]{0:T(128)} %slice.61.count_ref, s32[36]{0:T(128)} %convert_reduce_fusion.9.group_ref, s32[72]{0:T(128)} %copy-done.26, s32[72]{0:T(128)} %and_select_fusion.3.steps_ref, s32[4,32,128]{2,1,0:T(8,128)} %fusion.18.pos_ref, f32[4,32,128]{2,1,0:T(8,128)} %reshape_reshape.13.prob_ref, ...), custom_call_target="tpu_custom_call" | custom-call | flops 22000001024 | bytes 45000000 | tf_op jit(solution)/shard_map/dispatch/pallas_call | solution.py:135
  824.3 117.4 %backward.3 = (bf16[9216,2816]{1,0:T(8,128)(2,1)}, bf16[9216,2048]{1,0:T(8,128)(2,1)}, bf16[9216,2048]{1,0:T(8,128)(2,1)}, f32[9216,128]{1,0:T(8,128)}) custom-call(s32[1]{0:T(128)} %slice.61.count_ref, s32[36]{0:T(128)} %convert_reduce_fusion.9.group_ref, s32[1]{0:T(128)} %bitcast.8.base_ref, bf16[9216,2048]{1,0:T(8,128)(2,1)} %dispatch.7.m_hbm, ...), custom_call_target="tpu_custom_call" | custom-call | flops 95000002560 | bytes 220000000 | tf_op jit(solution)/shard_map/backward/pallas_call | solution.py:428
  941.8 31.5 %combine.7 = (bf16[4096,2048]{1,0:T(8,128)(2,1)}, f32[4096,128]{1,0:T(8,128)}) custom-call(s32[128]{0:T(128)} %reshape.302.start_ref, s32[5]{0:T(128)} %pad_add_fusion.1.first_ref, s32[32]{0:T(128)} %convert_element_type.180.over_ref, s32[1]{0:T(128)} %slice.61.count_ref, s32[4,32,128]{2,1,0:T(8,128)} %fusion.18.pos_ref, ...), custom_call_target="tpu_custom_call" | custom-call | flops 11000000512 | bytes 40000000 | tf_op jit(solution)/shard_map/combine/pallas_call | solution.py:262
  981.5 2.5 convert_element_type.179
  984.1 4.1 convert_element_type.183
  988.1 77.8 %weight_grad.3 = bf16[4,1408,2048]{2,1,0:T(8,128)(2,1)} custom-call(s32[5]{0:T(128)} %pad_add_fusion.begin_ref, s32[40]{0:T(128)} %get-tuple-element.123.src0_ref, s32[40]{0:T(128)} %get-tuple-element.122.src1_ref, s32[40]{0:T(128)} %compare_convert_fusion.pair_ref, bf16[9216,1408]{1,0:T(8,128)(2,1)} %get-tuple-element.51.h_hbm.la_hbm, ...), custom_call_target="tpu_custom_call" | custom-call | flops 57671680000 | bytes 100000000 | tf_op jit(solution)/shard_map/weight_grad/pallas_call | solution.py:525
  1066.0 150.4 %weight_grad.2 = (bf16[4,2048,1408]{2,1,0:T(8,128)(2,1)}, bf16[4,2048,1408]{2,1,0:T(8,128)(2,1)}) custom-call(s32[5]{0:T(128)} %pad_add_fusion.begin_ref, s32[40]{0:T(128)} %get-tuple-element.123.src0_ref, s32[40]{0:T(128)} %get-tuple-element.122.src1_ref, s32[40]{0:T(128)} %compare_convert_fusion.pair_ref, ...), custom_call_target="tpu_custom_call" | custom-call | flops 115343360000 | bytes 100000000 | tf_op jit(solution)/shard_map/weight_grad/pallas_call | solution.py:525
  1217.4 2.8 fusion.45
  1220.3 2.4 reduce-scatter.12.cloned.1.call-done
  1222.7 8.0 fusion.10
  1232.7 11.8 multiply_reduce_fusion
  1244.5 23.6 %all-reduce = (bf16[2048]{0:T(1024)(128)(2,1)}, bf16[2048,8]{0,1:T(8,128)(2,1)}, f32[]{:T(128)}) all-reduce(f32[2048]{0:T(1024)S(1)} %get-tuple-element.73, f32[2048,8]{0,1:T(8,128)S(1)} %fusion.45, f32[]{:T(128)} %get-tuple-element.109), channel_id=1, replica_groups=mesh['tp'=4,'ep'=2] {'tp','ep'}, use_global_device_ids=true, to_apply=%region_31.32 | all-reduce | flops 18433 | bytes 110600 | tf_op jit(solution)/shard_map/psum | solution.py:738
  (144 shorter events, 29.5 us)
Async XLA Ops:
  7.2 12.5 copy-start
  7.2 101.6 %all-gather.8.cloned.1.call-start = ((), (), s32[]{:S(2)}) async-start(), calls=%async_computation.6 | async-start | bytes 18874368 | tf_op jit(solution)/shard_map/all_gather | solution.py:650
  10.3 8.5 copy-start.14
  11.0 7.8 copy-start.10
  16.3 3.4 copy-start.16
  18.8 282.6 %all-gather.6.cloned.1.call-start = ((), (), s32[]{:S(2)}) async-start(), calls=%async_computation.5 | async-start | bytes 18874368 | tf_op jit(solution)/shard_map/all_gather | solution.py:650
  19.6 434.5 %reduce-scatter.6.cloned.1.call-start = ((), (), s32[]{:S(2)}) async-start(), calls=%async_computation.7 | async-start | bytes 18874368 | tf_op jit(solution)/shard_map/reduce_scatter | solution.py:653
  23.1 19.9 %copy-start.6 = (f32[1024,8]{0,1:T(8,128)}, f32[1024,8]{0,1:T(8,128)S(1)}, u32[]{:S(2)}) copy-start(f32[1024,8]{0,1:T(8,128)S(1)} %get-tuple-element.127) | copy-start | bytes 98308
  23.1 23.3 %copy-start.8 = (f32[1024]{0:T(1024)}, f32[1024]{0:T(1024)S(1)}, u32[]{:S(2)}) copy-start(f32[1024]{0:T(1024)S(1)} %get-tuple-element.126) | copy-start | bytes 12292
  43.9 9.9 copy-start.18
  52.4 56.4 %copy-start.27 = (s32[72]{0:T(128)}, s32[72]{0:T(128)S(1)}, u32[]{:S(2)}) copy-start(s32[72]{0:T(128)S(1)} %get-tuple-element.82.lo_ref) | copy-start | bytes 868
  52.4 247.6 %copy-start.26 = (s32[72]{0:T(128)}, s32[72]{0:T(128)S(1)}, u32[]{:S(2)}) copy-start(s32[72]{0:T(128)S(1)} %get-tuple-element.83.lo_ref) | copy-start | bytes 868
  298.7 244.2 %all-gather.10.cloned.1.call-start = ((), (), s32[]{:S(2)}) async-start(), calls=%async_computation.8 | async-start | bytes 18874368 | tf_op jit(solution)/shard_map/all_gather | solution.py:650
  454.1 4.6 copy-start.29
  454.1 5.1 copy-start.22
  458.7 242.9 %reduce-scatter.8.cloned.1.call-start = ((), (), s32[]{:S(2)}) async-start(), calls=%async_computation.9 | async-start | bytes 18874368 | tf_op jit(solution)/shard_map/reduce_scatter | solution.py:653
  542.9 247.4 %all-gather.12.cloned.1.call-start = ((), (), s32[]{:S(2)}) async-start(), calls=%async_computation.10 | async-start | bytes 18874368 | tf_op jit(solution)/shard_map/all_gather | solution.py:650
  706.0 510.4 %reduce-scatter.14.cloned.1.call-start = ((), (), s32[]{:S(2)}) async-start(), calls=%async_computation.13 | async-start | bytes 294912 | tf_op jit(solution)/shard_map/reduce_scatter | solution.py:653
  976.2 244.1 %reduce-scatter.10.cloned.1.call-start = ((), (), s32[]{:S(2)}) async-start(), calls=%async_computation.11 | async-start | bytes 18874368 | tf_op jit(solution)/shard_map/reduce_scatter | solution.py:653
  976.9 245.7 %reduce-scatter.12.cloned.1.call-start = ((), (), s32[]{:S(2)}) async-start(), calls=%async_computation.12 | async-start | bytes 18874368 | tf_op jit(solution)/shard_map/reduce_scatter | solution.py:653
  977.0 3.2 copy-start.19
  977.0 3.2 copy-start.23
  977.1 4.5 copy-start.5
  1066.0 151.3 %copy-start.7 = (f32[1024,8]{0,1:T(8,128)S(1)}, f32[1024,8]{0,1:T(8,128)}, u32[]{:S(2)}) copy-start(f32[1024,8]{0,1:T(8,128)} %copy-done.6) | copy-start | bytes 98308
  1066.0 151.2 %copy-start.9 = (f32[1024]{0:T(1024)S(1)}, f32[1024]{0:T(1024)}, u32[]{:S(2)}) copy-start(f32[1024]{0:T(1024)} %copy-done.8) | copy-start | bytes 12292
  1066.0 151.2 %copy-start.13 = (f32[1024]{0:T(1024)S(1)}, f32[1024]{0:T(1024)}, u32[]{:S(2)}) copy-start(f32[1024]{0:T(1024)} %copy-done.12) | copy-start | bytes 12292
  1066.0 151.2 %copy-start.17 = (f32[8]{0:T(128)S(1)}, f32[8]{0:T(128)}, u32[]{:S(2)}) copy-start(f32[8]{0:T(128)} %get-tuple-element.125) | copy-start | bytes 100
  1066.0 156.7 %copy-start.11 = (f32[2048]{0:T(1024)S(1)}, f32[2048]{0:T(1024)}, u32[]{:S(2)}) copy-start(f32[2048]{0:T(1024)} %copy-done.10) | copy-start | bytes 24580
  1066.0 156.6 %copy-start.15 = (f32[1024]{0:T(1024)S(1)}, f32[1024]{0:T(1024)}, u32[]{:S(2)}) copy-start(f32[1024]{0:T(1024)} %copy-done.14) | copy-start | bytes 12292
  1222.7 8.0 copy-start.2
  1222.7 8.4 copy-start.3
  1222.7 10.0 copy-start.4
  (7 other events, 11.3 us)
Sparse Core Ops, SparseCore 0:
  18.9 89.7 all-gather.7
  111.2 84.0 all-gather.5
  298.8 106.9 reduce-scatter.5
  458.8 84.0 all-gather.9
  546.8 106.9 reduce-scatter.7
  706.2 84.0 all-gather.11
  976.3 25.3 reduce-scatter.13
  1005.2 106.9 reduce-scatter.9
  1115.7 106.9 reduce-scatter.11
